TPU v7x, 32 devices: a whole 2x2x4 slice. The times are simulated.
32 devices in a mesh: section: 4 (over y, core), expert: 8 (over z, x).
Axes of the slice: x: 2, y: 2, z: 4, core: 2. Of those that a mesh axis runs over, the one named last changes fastest.
Arguments:
- inputs: bfloat16 [4, 1024, 1024], P('section', 'expert'), may hold values from -6 to 6
- out_grads: bfloat16 [4, 1024, 1024], P('section', 'expert'), may hold values from -6 to 6
- expert_ids: int32 [4, 1024, 8], P('section', 'expert'), may hold values from 0 to 15, all different within a row; in each aligned block of 128 rows (0 to 127, 128 to 255, ..., all dimensions but the last counted through in order) at most 96 rows name the same one
- route_levels: int32 [4, 1024, 8], P('section', 'expert'), may hold values from 8 to 256
- w_gate: bfloat16 [4, 16, 1024, 384], P('section', 'expert'), may hold values from -0.1875 to 0.1875
- w_up: bfloat16 [4, 16, 1024, 384], P('section', 'expert'), may hold values from -0.1875 to 0.1875
- w_down: bfloat16 [4, 16, 384, 1024], P('section', 'expert'), may hold values from -0.3125 to 0.3125
Outputs:
- upstream: bfloat16 [4, 1024, 1024], P('section', 'expert')
- route_grad: bfloat16 [4, 1024, 8], P('section', 'expert')
- gate_update: bfloat16 [4, 16, 1024, 384], P('section', 'expert')
- up_update: bfloat16 [4, 16, 1024, 384], P('section', 'expert')
- down_update: bfloat16 [4, 16, 384, 1024], P('section', 'expert')
Inputs may be any that keep to these rules, and one draw needn't show every extreme that they name: `expert_ids`: each token names 8 different experts; among the 128 tokens of one aligned block no expert is named more than 96 times.
All inputs are finite; a program needn't handle non-finite values.
Results may differ from a plain program's by a relative error of at most 0.0064.
Values may be sent and summed in bfloat16 or wider, within the bound.
A program may use at most 128 MiB of HBM per device.

v0:
```python
import jax
import jax.numpy as jnp
from jax import lax
from jax.sharding import PartitionSpec as P


def shifted(value, axis, by):
    size = lax.axis_size(axis)
    pairs = [(i, i + by) for i in range(size) if 0 <= i + by < size]
    return lax.ppermute(value, axis, pairs)


def flat_slots(expert_ids, experts_all, capacity):
    blocks = expert_ids.shape[0]
    flat_ids = expert_ids.reshape(blocks, -1)
    catalog = jnp.arange(experts_all, dtype=jnp.int32)
    onehot = (flat_ids[:, :, None] == catalog[None, None, :]).astype(jnp.int32)
    rank_table = jnp.cumsum(onehot, axis=1) - 1
    slot_of = jnp.sum(onehot * rank_table, axis=2)
    return (flat_ids * capacity + slot_of).reshape(expert_ids.shape)


def expert_backward(slot_inputs, slot_grads, slot_routes, w_gate, w_up, w_down):
    gate_pre = jnp.einsum("esd,edh->esh", slot_inputs, w_gate, preferred_element_type=jnp.float32)
    up_pre = jnp.einsum("esd,edh->esh", slot_inputs, w_up, preferred_element_type=jnp.float32)
    sigmoid_gate = jax.nn.sigmoid(gate_pre)
    silu_gate = gate_pre * sigmoid_gate
    active = (silu_gate * up_pre).astype(jnp.bfloat16)
    expert_out = jnp.einsum("esh,ehd->esd", active, w_down, preferred_element_type=jnp.float32)
    route_part = jnp.sum(slot_grads.astype(jnp.float32) * expert_out, axis=2).astype(jnp.bfloat16)
    weighted = (
        slot_routes.astype(jnp.float32)[:, :, None] * slot_grads.astype(jnp.float32)
    ).astype(jnp.bfloat16)
    active_grad = jnp.einsum("esd,ehd->esh", weighted, w_down, preferred_element_type=jnp.float32)
    gate_pre_grad = (
        active_grad * up_pre * sigmoid_gate * (1.0 + gate_pre * (1.0 - sigmoid_gate))
    ).astype(jnp.bfloat16)
    up_pre_grad = (active_grad * silu_gate).astype(jnp.bfloat16)
    input_grad = (
        jnp.einsum("esh,edh->esd", gate_pre_grad, w_gate, preferred_element_type=jnp.float32)
        + jnp.einsum("esh,edh->esd", up_pre_grad, w_up, preferred_element_type=jnp.float32)
    ).astype(jnp.bfloat16)
    down_part = jnp.einsum(
        "esh,esd->ehd", active, weighted, preferred_element_type=jnp.float32
    ).astype(jnp.bfloat16)
    gate_part = jnp.einsum(
        "esd,esh->edh", slot_inputs, gate_pre_grad, preferred_element_type=jnp.float32
    ).astype(jnp.bfloat16)
    up_part = jnp.einsum(
        "esd,esh->edh", slot_inputs, up_pre_grad, preferred_element_type=jnp.float32
    ).astype(jnp.bfloat16)
    return (input_grad, route_part, gate_part, up_part, down_part)


def body(inputs, out_grads, expert_ids, route_levels, w_gate, w_up, w_down):
    tok_rows = inputs.shape[1]
    width = inputs.shape[2]
    top_count = expert_ids.shape[2]
    experts_local = w_gate.shape[1]
    groups = lax.axis_size("expert")
    experts_all = experts_local * groups
    capacity = 3 * tok_rows * top_count // (2 * experts_all)
    slot_total = experts_all * capacity
    own_index = flat_slots(expert_ids[0][None], experts_all, capacity)[0]
    catalog = jnp.arange(slot_total, dtype=jnp.int32)
    select = (own_index[:, :, None] == catalog).astype(jnp.bfloat16)
    placing = jnp.sum(select, axis=1)
    route_values = (route_levels[0].astype(jnp.float32) / 256.0).astype(jnp.bfloat16)
    all_inputs, all_grads, all_routes, all_choices = (
        lax.all_gather(inputs[0], "expert", axis=0, tiled=True),
        lax.all_gather(out_grads[0], "expert", axis=0, tiled=True),
        lax.all_gather(route_values, "expert", axis=0, tiled=True),
        lax.all_gather(expert_ids[0].astype(jnp.bfloat16), "expert", axis=0, tiled=True),
    )
    source_ids = all_choices.astype(jnp.int32).reshape(groups, tok_rows, top_count)
    first_expert = lax.axis_index("expert") * experts_local
    local_index = flat_slots(source_ids, experts_all, capacity) - first_expert * capacity
    local_catalog = jnp.arange(experts_local * capacity, dtype=jnp.int32)
    local_select = (
        (local_index[..., None] == local_catalog)
        .astype(jnp.bfloat16)
        .reshape(groups, tok_rows, top_count, experts_local, capacity)
    )
    local_placing = jnp.sum(local_select, axis=2)
    slot_inputs = (
        jnp.einsum(
            "ntec,ntd->encd",
            local_placing,
            all_inputs.reshape(groups, tok_rows, width),
            preferred_element_type=jnp.float32,
        )
        .astype(jnp.bfloat16)
        .reshape(experts_local, groups * capacity, width)
    )
    slot_grads = (
        jnp.einsum(
            "ntec,ntd->encd",
            local_placing,
            all_grads.reshape(groups, tok_rows, width),
            preferred_element_type=jnp.float32,
        )
        .astype(jnp.bfloat16)
        .reshape(experts_local, groups * capacity, width)
    )
    slot_routes = (
        jnp.einsum(
            "ntkec,ntk->enc",
            local_select,
            all_routes.reshape(groups, tok_rows, top_count),
            preferred_element_type=jnp.float32,
        )
        .astype(jnp.bfloat16)
        .reshape(experts_local, groups * capacity)
    )
    input_grad, route_part, gate_part, up_part, down_part = expert_backward(
        slot_inputs, slot_grads, slot_routes, w_gate[0], w_up[0], w_down[0]
    )
    back_inputs, back_routes = (
        lax.all_to_all(input_grad, "expert", split_axis=1, concat_axis=0, tiled=True),
        lax.all_to_all(route_part, "expert", split_axis=1, concat_axis=0, tiled=True),
    )
    token_grad = jnp.dot(
        placing, back_inputs.reshape(slot_total, width), preferred_element_type=jnp.float32
    ).astype(jnp.bfloat16)
    token_route = jnp.einsum(
        "tks,s->tk", select, back_routes.reshape(slot_total), preferred_element_type=jnp.float32
    ).astype(jnp.bfloat16)
    upstream = shifted(token_grad, "section", -1)
    return (upstream[None], token_route[None], gate_part[None], up_part[None], down_part[None])


def solution(mesh):
    in_specs = (
        P("section", "expert", None),
        P("section", "expert", None),
        P("section", "expert", None),
        P("section", "expert", None),
        P("section", "expert", None, None),
        P("section", "expert", None, None),
        P("section", "expert", None, None),
    )
    out_specs = (
        P("section", "expert", None),
        P("section", "expert", None),
        P("section", "expert", None, None),
        P("section", "expert", None, None),
        P("section", "expert", None, None),
    )
    return jax.shard_map(body, mesh=mesh, in_specs=in_specs, out_specs=out_specs, check_vma=False)
```

profile of v0, /device:TPU:1, one launch (start us, length us, event | category | flops | bytes accessed | tf_op | source)
XLA Modules:
  0.0 240.5 jit_solution(3943738356832630842)
XLA Ops:
  9.4 23.1 %all-gather.1 = bf16[1,1024,8]{1,2,0:T(8,128)(2,1)S(1)} all-gather(bf16[1,128,8]{1,2,0:T(8,128)(2,1)S(1)} %convert_element_type.122), channel_id=3, replica_groups=mesh['section'=4,'expert'=8] {'expert'}, dimensions={1}, use_global_device_ids=true | all-gather | bytes 18432 | tf_op jit(solution)/shard_map/all_gather | solution.py:73
  33.4 36.0 %reduce-window.16 = s32[8,16,8,128]{3,2,1,0:T(8,128)S(1)} reduce-window(s32[8,16,8,128]{3,2,1,0:T(8,128)S(1)} %fusion.23, s32[]{:T(128)} %constant.30.clone.1), window={size=1x1x1x128 pad=0_0x0_0x0_0x127_0}, to_apply=%region_4.5 | reduce-window | flops 16646144 | bytes 1048580 | tf_op jit(solution)/shard_map/reduce-window.2
  71.2 22.5 %all-gather = bf16[1,1024,8]{1,2,0:T(8,128)(2,1)S(1)} all-gather(bf16[1,128,8]{1,2,0:T(8,128)(2,1)S(1)} %multiply_convert_fusion.3), channel_id=2, replica_groups=mesh['section'=4,'expert'=8] {'expert'}, dimensions={1}, use_global_device_ids=true | all-gather | bytes 18432 | tf_op jit(solution)/shard_map/all_gather | solution.py:72
  93.7 1.1 fusion.4
  95.0 0.7 convert_reduce_fusion
  95.7 2.6 %convert_bitcast_fusion.1 = bf16[2,8,96,1024]{3,2,0,1:T(8,128)(2,1)S(1)} fusion(bf16[8,128,2,96]{1,3,2,0:T(8,128)(2,1)S(1)} %convert_reduce_fusion, bf16[8,128,1024,1]{2,1,3,0:T(8,128)(2,1)} %bitcast.118), kind=kOutput, calls=%fused_computation.12 | convolution fusion | flops 404226048 | bytes 5636096 | tf_op jit(solution)/shard_map/ntec,ntd->encd/dot_general | solution.py:86
  98.3 2.1 copy.95
  100.4 10.0 %all-gather.7.cloned.1.call-done = bf16[1,1024,1024]{2,1,0:T(8,128)(2,1)} async-done(((bf16[1,128,1024]{2,1,0:T(8,128)(2,1)}), bf16[1,1024,1024]{2,1,0:T(8,128)(2,1)}) %all-gather.7.cloned.1.call-update) | async-done | bytes 2097168 | tf_op jit(solution)/shard_map/all_gather | solution.py:71
  110.4 2.6 %convert_bitcast_fusion = f32[2,8,96,1024]{3,2,0,1:T(8,128)S(1)} fusion(bf16[8,128,2,96]{1,3,2,0:T(8,128)(2,1)S(1)} %convert_reduce_fusion, bf16[8,128,1024,1]{2,1,3,0:T(8,128)(2,1)} %bitcast.112), kind=kOutput, calls=%fused_computation.4 | convolution fusion | flops 405798912 | bytes 8781824 | tf_op jit(solution)/shard_map/ntec,ntd->encd/dot_general | solution.py:96
  112.9 1.1 copy.94
  114.1 0.7 copy-done.1
  115.3 1.8 fusion.11
  117.5 1.0 copy-done.4
  118.5 1.8 fusion.17
  120.3 4.2 %multiply_convert_fusion = (bf16[2,768,384]{2,1,0:T(8,128)(2,1)S(1)}, bf16[2,768,384]{2,1,0:T(8,128)(2,1)}, bf16[2,768,384]{2,1,0:T(8,128)(2,1)}) fusion(f32[2,768,384]{2,1,0:T(8,128)S(1)} %fusion.11, f32[2,768,384]{2,1,0:T(8,128)S(1)} %fusion.17, bf16[2,768,1024]{2,1,0:T(8,128)(2,1)S(1)} %bitcast.114, bf16[1,2,1024,384]{3,2,1,0:T(8,128)(2,1)S(1)} %copy-done), kind=kOutput, calls=%fused_computation.16 | convolution fusion | flops 1216806912 | bytes 12976128 | tf_op jit(solution)/shard_map/esd,edh->esh/dot_general | solution.py:25
  124.5 1.0 copy-done.9
  125.5 1.9 fusion.1
  128.1 3.7 %all-to-all-start.1 = ((bf16[2,8,96]{2,0,1:T(2,128)(2,1)}), bf16[2,8,96]{2,0,1:T(2,128)(2,1)S(1)}, u32[]{:S(2)}, u32[]{:S(2)}) async-start(bf16[2,8,96]{2,0,1:T(2,128)(2,1)} %copy.99), calls=%async_computation.1 | async-start | bytes 8192 | tf_op jit(solution)/shard_map/all_to_all | solution.py:120
  131.8 3.2 %fusion.9 = f32[2,768,1024]{2,1,0:T(8,128)S(1)} fusion(bf16[2,768,384]{2,1,0:T(8,128)(2,1)} %get-tuple-element.6, bf16[1,2,1024,384]{3,2,1,0:T(8,128)(2,1)S(1)} %copy-done.5), kind=kOutput, calls=%fused_computation.24 | convolution fusion | flops 1207959552 | bytes 9043968 | tf_op jit(solution)/shard_map/esh,edh->esd/dot_general | solution.py:40
  135.0 1.8 add_convert_fusion
  136.9 4.9 %copy.96 = bf16[2,768,1024]{2,0,1:T(2,128)(2,1)} copy(bf16[2,768,1024]{2,1,0:T(8,128)(2,1)S(1)} %add_convert_fusion) | data formatting | bytes 6291456 | tf_op jit(solution)/shard_map/convert_element_type | solution.py:42
  141.8 5.6 %all-to-all-start = ((bf16[2,768,1024]{2,0,1:T(2,128)(2,1)}), bf16[2,768,1024]{2,0,1:T(2,128)(2,1)}, u32[]{:S(2)}, u32[]{:S(2)}) async-start(bf16[2,768,1024]{2,0,1:T(2,128)(2,1)} %copy.96), calls=%async_computation | async-start | bytes 6291456 | tf_op jit(solution)/shard_map/all_to_all | solution.py:119
  147.6 4.5 %reduce-window.14 = s32[1,16,8,128]{3,2,1,0:T(8,128)S(1)} reduce-window(s32[1,16,8,128]{3,2,1,0:T(8,128)S(1)} %bitcast.120, s32[]{:T(128)} %constant.30.clone.1), window={size=1x1x1x128 pad=0_0x0_0x0_0x127_0}, to_apply=%region_0.0 | reduce-window | flops 2080768 | bytes 131076 | tf_op jit(solution)/shard_map/reduce-window
  152.7 3.1 %fusion.6 = bf16[128,1536]{1,0:T(8,128)(2,1)S(1)} fusion(s32[128,8]{1,0:T(8,128)S(1)} %bitcast_add_fusion), kind=kLoop, calls=%fused_computation.11 | loop fusion | flops 4521984 | bytes 397312 | tf_op jit(solution)/shard_map/reduce_sum | solution.py:67
  155.9 4.6 %fusion.21 = bf16[1,2,384,1024]{3,2,1,0:T(8,128)(2,1)} fusion(bf16[2,768,384]{2,1,0:T(8,128)(2,1)S(1)} %copy-done.10, bf16[2,768,1024]{2,1,0:T(8,128)(2,1)} %copy-done.3), kind=kOutput, calls=%fused_computation.36 | convolution fusion | flops 1208745984 | bytes 5898240 | tf_op jit(solution)/shard_map/esh,esd->ehd/dot_general | solution.py:43
  160.5 3.0 %fusion.19 = bf16[1,2,1024,384]{3,2,1,0:T(8,128)(2,1)} fusion(bf16[2,768,1024]{2,1,0:T(8,128)(2,1)S(1)} %bitcast.115, bf16[2,768,384]{2,1,0:T(8,128)(2,1)S(1)} %copy-done.8), kind=kOutput, calls=%fused_computation.34 | convolution fusion | flops 1208745984 | bytes 5898240 | tf_op jit(solution)/shard_map/esd,esh->edh/dot_general | solution.py:46
  163.5 3.0 %fusion.20 = bf16[1,2,1024,384]{3,2,1,0:T(8,128)(2,1)} fusion(bf16[2,768,1024]{2,1,0:T(8,128)(2,1)S(1)} %bitcast.116, bf16[2,768,384]{2,1,0:T(8,128)(2,1)S(1)} %copy-done.7), kind=kOutput, calls=%fused_computation.35 | convolution fusion | flops 1208745984 | bytes 5898240 | tf_op jit(solution)/shard_map/esd,esh->edh/dot_general | solution.py:49
  166.6 49.5 %all-to-all-done = bf16[2,768,1024]{2,0,1:T(2,128)(2,1)} async-done(((bf16[2,768,1024]{2,0,1:T(2,128)(2,1)}), bf16[2,768,1024]{2,0,1:T(2,128)(2,1)}, u32[]{:S(2)}, u32[]{:S(2)}) %all-to-all-start) | async-done | bytes 3145760 | tf_op jit(solution)/shard_map/all_to_all | solution.py:119
  216.1 2.8 %copy.97 = bf16[2,768,1024]{2,1,0:T(8,128)(2,1)S(1)} copy(bf16[2,768,1024]{2,0,1:T(2,128)(2,1)} %all-to-all-done) | data formatting | bytes 6291456 | tf_op jit(solution)/shard_map/all_to_all | solution.py:119
  219.9 5.2 %collective-permute-start = (bf16[128,1024]{1,0:T(8,128)(2,1)S(1)}, bf16[128,1024]{1,0:T(8,128)(2,1)S(1)}, u32[]{:S(2)}, u32[]{:S(2)}) collective-permute-start(bf16[128,1024]{1,0:T(8,128)(2,1)S(1)} %convolution_convert_fusion.3), channel_id=1, source_target_pairs={{8,0},{16,8},{24,16},{9,1},{17,9},{25,17},{10,2},{18,10},{26,18},{... | collective-permute-start | bytes 786440 | tf_op jit(solution)/shard_map/ppermute | solution.py:10
  225.2 7.1 %fusion.2 = bf16[1,128,8]{2,0,1:T(2,128)(2,1)S(1)} fusion(bf16[1536,1,1]{0,1,2:T(2,128)(2,1)S(1)} %reshape.250, s32[128,8]{1,0:T(8,128)S(1)} %bitcast_add_fusion), kind=kOutput, calls=%fused_computation.7 | convolution fusion | flops 4718592 | bytes 9216 | tf_op jit(solution)/shard_map/tks,s->tk/dot_general | solution.py:125
  232.9 0.7 copy.121
  (76 shorter events, 9.1 us)
Async XLA Ops:
  7.2 113.1 %copy-start = (bf16[1,2,1024,384]{3,2,1,0:T(8,128)(2,1)S(1)}, bf16[1,2,1024,384]{3,2,1,0:T(8,128)(2,1)}, u32[]{:S(2)}) copy-start(bf16[1,2,1024,384]{3,2,1,0:T(8,128)(2,1)} %param.12) | copy-start | bytes 4718596
  7.2 88.5 %all-gather.9.cloned.1.call-start = ((), (), s32[]{:S(2)}) async-start(), calls=%async_computation.3 | async-start | bytes 2359296 | tf_op jit(solution)/shard_map/all_gather | solution.py:70
  7.9 102.4 %all-gather.7.cloned.1.call-start = ((), (), s32[]{:S(2)}) async-start(), calls=%async_computation.2 | async-start | bytes 2359296 | tf_op jit(solution)/shard_map/all_gather | solution.py:71
  70.5 0.8 copy-start.12
  112.9 1.9 copy-start.1
  112.9 2.3 copy-start.5
  117.1 1.4 copy-start.4
  118.5 1.8 copy-start.3
  124.5 1.0 copy-start.9
  128.1 13.7 %all-to-all-start.1 = ((bf16[2,8,96]{2,0,1:T(2,128)(2,1)}), bf16[2,8,96]{2,0,1:T(2,128)(2,1)S(1)}, u32[]{:S(2)}, u32[]{:S(2)}) async-start(bf16[2,8,96]{2,0,1:T(2,128)(2,1)} %copy.99), calls=%async_computation.1 | async-start | bytes 8192 | tf_op jit(solution)/shard_map/all_to_all | solution.py:120
  131.8 3.2 %copy-start.6 = (bf16[2,768,384]{2,1,0:T(8,128)(2,1)S(1)}, bf16[2,768,384]{2,1,0:T(8,128)(2,1)}, u32[]{:S(2)}) copy-start(bf16[2,768,384]{2,1,0:T(8,128)(2,1)} %get-tuple-element.7) | copy-start | bytes 3538948
  141.8 5.6 %copy-start.11 = (s32[1,128,8]{1,2,0:T(8,128)S(1)}, s32[1,128,8]{1,2,0:T(8,128)}, u32[]{:S(2)}) copy-start(s32[1,128,8]{1,2,0:T(8,128)} %param.9) | copy-start | bytes 12292
  141.8 14.1 %copy-start.10 = (bf16[2,768,384]{2,1,0:T(8,128)(2,1)S(1)}, bf16[2,768,384]{2,1,0:T(8,128)(2,1)}, u32[]{:S(2)}) copy-start(bf16[2,768,384]{2,1,0:T(8,128)(2,1)} %copy-done.9) | copy-start | bytes 3538948
  141.8 74.3 %all-to-all-start = ((bf16[2,768,1024]{2,0,1:T(2,128)(2,1)}), bf16[2,768,1024]{2,0,1:T(2,128)(2,1)}, u32[]{:S(2)}, u32[]{:S(2)}) async-start(bf16[2,768,1024]{2,0,1:T(2,128)(2,1)} %copy.96), calls=%async_computation | async-start | bytes 6291456 | tf_op jit(solution)/shard_map/all_to_all | solution.py:119
  155.9 4.6 %copy-start.2 = (bf16[2,8,96,1024]{3,2,1,0:T(8,128)(2,1)S(1)}, bf16[2,8,96,1024]{3,2,1,0:T(8,128)(2,1)}, u32[]{:S(2)}) copy-start(bf16[2,8,96,1024]{3,2,1,0:T(8,128)(2,1)} %copy.95) | copy-start | bytes 9437188
  155.9 4.6 %copy-start.8 = (bf16[2,768,384]{2,1,0:T(8,128)(2,1)S(1)}, bf16[2,768,384]{2,1,0:T(8,128)(2,1)}, u32[]{:S(2)}) copy-start(bf16[2,768,384]{2,1,0:T(8,128)(2,1)} %get-tuple-element.6) | copy-start | bytes 3538948
  160.5 3.0 %copy-start.7 = (bf16[2,768,384]{2,1,0:T(8,128)(2,1)S(1)}, bf16[2,768,384]{2,1,0:T(8,128)(2,1)}, u32[]{:S(2)}) copy-start(bf16[2,768,384]{2,1,0:T(8,128)(2,1)} %get-tuple-element.7) | copy-start | bytes 3538948
  219.9 13.0 %collective-permute-start = (bf16[128,1024]{1,0:T(8,128)(2,1)S(1)}, bf16[128,1024]{1,0:T(8,128)(2,1)S(1)}, u32[]{:S(2)}, u32[]{:S(2)}) collective-permute-start(bf16[128,1024]{1,0:T(8,128)(2,1)S(1)} %convolution_convert_fusion.3), channel_id=1, source_target_pairs={{8,0},{16,8},{24,16},{9,1},{17,9},{25,17},{10,2},{18,10},{26,18},{... | collective-permute-start | bytes 786440 | tf_op jit(solution)/shard_map/ppermute | solution.py:10
Sparse Core Ops, SparseCore 0:
  10.1 50.0 all-gather.8
  62.3 47.9 all-gather.6
where the time goes:
time: 241 us; the launch traced here: 240 us
  waiting for transfers between devices  60.9 us (25%)
  other arithmetic  46 us (19%)
  blocking collectives  45.6 us (19%)
  matrix products  39.2 us (16%)
  local copies, waits for them, and re-layouts  19.8 us (8%)
  starting transfers between devices  14.6 us (6%)
  between operations  14.4 us (6%)
    all_to_all x1, waiting for transfers between devices, body(): lax.all_to_all(input_grad, 'expert', split_axis=1, concat_axis=0, tiled=T...  49.5 us
    another operation x4, other arithmetic  40.6 us
    all_gather x1, blocking collectives, body(): lax.all_gather(expert_ids[0].astype(jnp.bfloat16), 'expert', axis=0, tile...  23.1 us
    all_gather x1, blocking collectives, body(): lax.all_gather(route_values, 'expert', axis=0, tiled=True)  22.5 us
    all_gather x1, waiting for transfers between devices, body(): lax.all_gather(out_grads[0], 'expert', axis=0, tiled=True)  9.99 us
    dot_general x1, matrix products, body(): jnp.einsum('tks,s->tk', select, back_routes.reshape(slot_total), preferre...  7.06 us
    all_to_all x1, starting transfers between devices, body(): lax.all_to_all(input_grad, 'expert', split_axis=1, concat_axis=0, tiled=T...  5.56 us
    ppermute x1, starting transfers between devices, shifted(): return lax.ppermute(value, axis, pairs)  5.24 us
  transfers between devices with their start and end apart: 5, of which 2 were waited for; matrix products, arithmetic and copies ran while one was open for 34% of the time, Pallas kernels for 0%

commit v1 on v0

v1 whole, which is shorter than its diff:
```python
import functools
import math

import jax
import jax.numpy as jnp
from jax import lax
from jax.experimental import pallas as pl
from jax.experimental.pallas import tpu as pltpu
from jax.sharding import PartitionSpec as P

MESH = pl.DeviceIdType.MESH
INFO = 128


def kernel(
    lines, rows, sections,
    in_ref, grad_ref, route_ref, wg_ref, wu_ref, wd_ref,
    up_ref, own_route_ref, gate_ref, up_out_ref, down_ref,
    packed, w_in, w_down, hidden_grads, scaled_all, x_out, x_in, z_out, z_in, token,
    load_sem, weight_sem, store_sem,
    az_send, ax_send, a_recv, rx_send, rx_recv, rz_send, rz_recv, y_send, y_recv,
):
    blocks = lines * rows
    tok, width = in_ref.shape
    local, _, hidden = wg_ref.shape
    me = lax.axis_index("expert")
    section = lax.axis_index("section")
    z, x = me // rows, lax.rem(me, rows)

    def at(dz, dx):
        return lax.rem(z + dz, lines) * rows + lax.rem(x + dx, rows)

    loads = [
        pltpu.make_async_copy(in_ref, packed.at[me, :, pl.ds(0, width)], load_sem.at[0]),
        pltpu.make_async_copy(grad_ref, packed.at[me, :, pl.ds(width, width)], load_sem.at[1]),
        pltpu.make_async_copy(route_ref, packed.at[me, :, pl.ds(2 * width, INFO)], load_sem.at[2]),
    ]
    weights = []
    for e in range(local):
        weights.append((wg_ref.at[e], w_in.at[:, pl.ds(2 * e * hidden, hidden)]))
        weights.append((wu_ref.at[e], w_in.at[:, pl.ds((2 * e + 1) * hidden, hidden)]))
        weights.append((wd_ref.at[e], w_down.at[pl.ds(e * hidden, hidden), :]))
    weights = [pltpu.make_async_copy(a, b, weight_sem.at[i]) for i, (a, b) in enumerate(weights)]
    for copy in loads + weights:
        copy.start()

    barrier = pltpu.get_barrier_semaphore()
    for dz in range(1, lines):
        pl.semaphore_signal(barrier, inc=1, device_id={"expert": at(dz, 0)}, device_id_type=MESH)
    for dx in range(1, rows):
        pl.semaphore_signal(barrier, inc=1, device_id={"expert": at(0, dx)}, device_id_type=MESH)
    before = lax.rem(section + sections - 1, sections)
    after = lax.rem(section + 1, sections)
    for other in (before, after):
        pl.semaphore_signal(barrier, inc=1, device_id={"section": other}, device_id_type=MESH)
    pl.semaphore_wait(barrier, lines + rows)

    def gather_z(dz):
        return pltpu.make_async_remote_copy(
            src_ref=packed.at[me], dst_ref=packed.at[me],
            send_sem=az_send.at[dz], recv_sem=a_recv.at[me],
            device_id={"expert": at(dz, 0)}, device_id_type=MESH,
        )

    def gather_x(dz, dx):
        block = at(dz, 0)
        return pltpu.make_async_remote_copy(
            src_ref=packed.at[block], dst_ref=packed.at[block],
            send_sem=ax_send.at[dz, dx], recv_sem=a_recv.at[block],
            device_id={"expert": at(0, dx)}, device_id_type=MESH,
        )

    def arrived(block):
        pltpu.make_async_remote_copy(
            src_ref=packed.at[block], dst_ref=packed.at[block],
            send_sem=az_send.at[0], recv_sem=a_recv.at[block],
            device_id={"expert": at(1, 0)}, device_id_type=MESH,
        ).wait_recv()

    def reduce_x(dz, dx):
        line = lax.rem(z + dz, lines)
        return pltpu.make_async_remote_copy(
            src_ref=x_out.at[line, dx - 1], dst_ref=x_in.at[line, dx - 1],
            send_sem=rx_send.at[line, dx - 1], recv_sem=rx_recv.at[line, dx - 1],
            device_id={"expert": at(0, dx)}, device_id_type=MESH,
        )

    def reduce_z(dz):
        line = lax.rem(z + dz, lines)
        return pltpu.make_async_remote_copy(
            src_ref=z_out.at[line], dst_ref=z_in.at[dz],
            send_sem=rz_send.at[dz], recv_sem=rz_recv.at[dz],
            device_id={"expert": at(dz, 0)}, device_id_type=MESH,
        )

    for copy in loads:
        copy.wait()
    for dx in range(1, rows):
        gather_x(0, dx).start()
    for dz in range(1, lines):
        gather_z(dz).start()
    for copy in weights:
        copy.wait()

    catalog = lax.broadcasted_iota(jnp.int32, (tok, INFO), 1)
    first = me * local
    last_dims = (((1,), (1,)), ((), ()))

    def compute(block):
        route_all = packed[block, :, pl.ds(2 * width, INFO)].astype(jnp.float32)
        pre = jnp.dot(packed[block, :, pl.ds(0, width)], w_in[...], preferred_element_type=jnp.float32)
        back_all = lax.dot_general(
            packed[block, :, pl.ds(width, width)], w_down[...], last_dims,
            preferred_element_type=jnp.float32,
        )
        route_out = jnp.zeros((tok, INFO), jnp.float32)
        for e in range(local):
            mine = catalog == first + e
            route = jnp.sum(jnp.where(mine, route_all, 0.0), axis=1, keepdims=True)
            gate = pre[:, 2 * e * hidden : (2 * e + 1) * hidden]
            up = pre[:, (2 * e + 1) * hidden : (2 * e + 2) * hidden]
            back = back_all[:, e * hidden : (e + 1) * hidden]
            sig = jax.nn.sigmoid(gate)
            silu = gate * sig
            active = silu * up
            route_grad = jnp.sum(active * back, axis=1, keepdims=True)
            route_out = route_out + jnp.where(mine, route_grad, 0.0)
            back = back * route
            hidden_grads[block, :, pl.ds(2 * e * hidden, hidden)] = (
                back * up * sig * (1.0 + gate * (1.0 - sig))
            ).astype(jnp.bfloat16)
            hidden_grads[block, :, pl.ds((2 * e + 1) * hidden, hidden)] = (back * silu).astype(jnp.bfloat16)
            scaled_all[block, :, pl.ds(e * hidden, hidden)] = (active * route).astype(jnp.bfloat16)
        total = lax.dot_general(
            hidden_grads[block], w_in[...], last_dims, preferred_element_type=jnp.float32
        )
        return total.astype(jnp.bfloat16), route_out.astype(jnp.bfloat16)

    def send_line(dz):
        line = lax.rem(z + dz, lines)
        for dx in range(1, rows):
            reduce_x(dz, dx).wait_recv()
        value = z_out[line].astype(jnp.float32)
        for dx in range(1, rows):
            value = value + x_in[line, dx - 1].astype(jnp.float32)
        z_out[line] = value.astype(jnp.bfloat16)

    def step(j, carry):
        dz, dx = j // rows, lax.rem(j, rows)
        block = at(dz, dx)
        line = lax.rem(z + dz, lines)

        @pl.when(j > 0)
        def _():
            arrived(block)

        @pl.when((dx == 0) & (dz > 0))
        def _():
            for other in range(1, rows):
                gather_x(dz, other).start()

        total, route_out = compute(block)

        @pl.when(dx == 0)
        def _():
            z_out[line, :, pl.ds(0, width)] = total
            z_out[line, :, pl.ds(width, INFO)] = route_out

        @pl.when(dx > 0)
        def _():
            x_out[line, dx - 1, :, pl.ds(0, width)] = total
            x_out[line, dx - 1, :, pl.ds(width, INFO)] = route_out
            reduce_x(dz, dx).start()

        @pl.when((dx == 0) & (dz > 1))
        def _():
            send_line(dz - 1)
            reduce_z(dz - 1).start()

        return carry

    lax.fori_loop(0, blocks, step, 0)
    send_line(lines - 1)
    reduce_z(lines - 1).start()

    first_dims = (((0,), (0,)), ((), ()))
    all_rows = blocks * tok
    tile = 256 if width % 256 == 0 and (local * hidden) % 256 == 0 else 128

    @pl.loop(0, width // tile)
    def _(c):
        at_c = pl.ds(pl.multiple_of(c * tile, tile), tile)
        left = packed[:, :, at_c].reshape(all_rows, tile)
        right = hidden_grads[...].reshape(all_rows, 2 * local * hidden)
        w_in[at_c, :] = lax.dot_general(
            left, right, first_dims, preferred_element_type=jnp.float32
        ).astype(jnp.bfloat16)

    stores = []
    for e in range(local):
        stores.append((w_in.at[:, pl.ds(2 * e * hidden, hidden)], gate_ref.at[e]))
        stores.append((w_in.at[:, pl.ds((2 * e + 1) * hidden, hidden)], up_out_ref.at[e]))
    for e in range(local):
        stores.append((w_down.at[pl.ds(e * hidden, hidden), :], down_ref.at[e]))
    stores = [pltpu.make_async_copy(a, b, store_sem.at[i]) for i, (a, b) in enumerate(stores)]
    for copy in stores[: 2 * local]:
        copy.start()

    send_line(0)
    value = z_out[z].astype(jnp.float32)
    for dz in range(1, lines):
        reduce_z(dz).wait_recv()
        value = value + z_in[dz].astype(jnp.float32)
    token[...] = value[:, :width].astype(jnp.bfloat16)
    own_route_ref[...] = value[:, width:].astype(jnp.bfloat16)

    hop = pltpu.make_async_remote_copy(
        src_ref=token, dst_ref=up_ref, send_sem=y_send, recv_sem=y_recv,
        device_id={"section": before}, device_id_type=MESH,
    )

    @pl.when(section > 0)
    def _():
        hop.start()

    @pl.when(section == sections - 1)
    def _():
        up_ref[...] = jnp.zeros_like(up_ref)

    @pl.loop(0, local * hidden // tile)
    def _(c):
        at_c = pl.ds(pl.multiple_of(c * tile, tile), tile)
        left = scaled_all[:, :, at_c].reshape(all_rows, tile)
        right = packed[:, :, pl.ds(width, width)].reshape(all_rows, width)
        w_down[at_c, :] = lax.dot_general(
            left, right, first_dims, preferred_element_type=jnp.float32
        ).astype(jnp.bfloat16)

    for copy in stores[2 * local :]:
        copy.start()
    for dz in range(1, lines):
        gather_z(dz).wait_send()
        reduce_z(dz).wait_send()
    for dz in range(lines):
        for dx in range(1, rows):
            gather_x(dz, dx).wait_send()
            reduce_x(dz, dx).wait_send()

    @pl.when(section > 0)
    def _():
        hop.wait_send()

    @pl.when(section < sections - 1)
    def _():
        hop.wait_recv()

    for copy in stores:
        copy.wait()


def body(rows, inputs, out_grads, expert_ids, route_levels, w_gate, w_up, w_down):
    tok, width = inputs.shape[1:]
    local, _, hidden = w_gate.shape[1:]
    blocks = lax.axis_size("expert")
    sections = lax.axis_size("section")
    lines = blocks // rows
    catalog = jnp.arange(INFO, dtype=jnp.int32)
    chosen = expert_ids[0][:, :, None] == catalog
    levels = jnp.sum(jnp.where(chosen, route_levels[0][:, :, None], 0), axis=1)
    routes = (levels.astype(jnp.float32) / 256.0).astype(jnp.bfloat16)
    bf16 = jnp.bfloat16
    anywhere = pl.BlockSpec(memory_space=pl.ANY)
    inside = pl.BlockSpec(memory_space=pltpu.VMEM)
    dma = pltpu.SemaphoreType.DMA
    side = max(rows - 1, 1)
    upstream, own_routes, gates, ups, downs = pl.pallas_call(
        functools.partial(kernel, lines, rows, sections),
        out_shape=(
            jax.ShapeDtypeStruct((tok, width), bf16),
            jax.ShapeDtypeStruct((tok, INFO), bf16),
            jax.ShapeDtypeStruct(w_gate.shape[1:], bf16),
            jax.ShapeDtypeStruct(w_up.shape[1:], bf16),
            jax.ShapeDtypeStruct(w_down.shape[1:], bf16),
        ),
        in_specs=[anywhere] * 6,
        out_specs=(inside, inside, anywhere, anywhere, anywhere),
        scratch_shapes=[
            pltpu.VMEM((blocks, tok, 2 * width + INFO), bf16),
            pltpu.VMEM((width, 2 * local * hidden), bf16),
            pltpu.VMEM((local * hidden, width), bf16),
            pltpu.VMEM((blocks, tok, 2 * local * hidden), bf16),
            pltpu.VMEM((blocks, tok, local * hidden), bf16),
            pltpu.VMEM((lines, side, tok, width + INFO), bf16),
            pltpu.VMEM((lines, side, tok, width + INFO), bf16),
            pltpu.VMEM((lines, tok, width + INFO), bf16),
            pltpu.VMEM((lines, tok, width + INFO), bf16),
            pltpu.VMEM((tok, width), bf16),
            dma((3,)),
            dma((3 * local,)),
            dma((3 * local,)),
            dma((lines,)),
            dma((lines, rows)),
            dma((blocks,)),
            dma((lines, side)),
            dma((lines, side)),
            dma((lines,)),
            dma((lines,)),
            dma,
            dma,
        ],
        compiler_params=pltpu.CompilerParams(
            collective_id=0, has_side_effects=True, vmem_limit_bytes=66_000_000
        ),
    )(inputs[0], out_grads[0], routes, w_gate[0], w_up[0], w_down[0])
    token_route = jnp.sum(
        jnp.where(chosen, own_routes[:, None, :].astype(jnp.float32), 0.0), axis=2
    ).astype(bf16)
    return (upstream[None], token_route[None], gates[None], ups[None], downs[None])


def solution(mesh):
    blocks = mesh.shape["expert"]
    rows = math.isqrt(max(blocks // 2, 1))
    while blocks % rows:
        rows -= 1
    in_specs = (
        P("section", "expert", None),
        P("section", "expert", None),
        P("section", "expert", None),
        P("section", "expert", None),
        P("section", "expert", None, None),
        P("section", "expert", None, None),
        P("section", "expert", None, None),
    )
    out_specs = (
        P("section", "expert", None),
        P("section", "expert", None),
        P("section", "expert", None, None),
        P("section", "expert", None, None),
        P("section", "expert", None, None),
    )
    return jax.shard_map(
        functools.partial(body, rows), mesh=mesh, in_specs=in_specs, out_specs=out_specs, check_vma=False
    )
```

time: 241 us -> 142 us (0.59)
  Pallas kernels: 0 us -> 129 us
  waiting for transfers between devices: 60.9 us -> 0 us
  blocking collectives: 45.6 us -> 0 us
  other arithmetic: 46 us -> 2.12 us
  matrix products: 39.2 us -> 0 us
  starting transfers between devices: 14.6 us -> 0 us
  between operations: 14.4 us -> 0.65 us
  local copies, waits for them, and re-layouts: 19.8 us -> 9.85 us
    pallas_call x0 -> x1, Pallas kernels: none -> 129 us  [body(): pl.pallas_call(functools.partial(kernel, lines, rows, sections), out_shap...]
    all_to_all x2 -> x0, waiting for transfers between devices: 49.5 us -> none  [the longest x1 49.5 us: body(): lax.all_to_all(input_grad, 'expert', split_axis=1, concat_axis=0, tiled=T...]
    all_gather x2 -> x0, blocking collectives: 45.6 us -> none  [the longest x1 23.1 us: body(): lax.all_gather(expert_ids[0].astype(jnp.bfloat16), 'expert', axis=0, tile...]
    another operation x4 -> x0, other arithmetic: 40.6 us -> none
    dot_general x14 -> x0, matrix products: 39.2 us -> none  [the longest x1 7.06 us: body(): jnp.einsum('tks,s->tk', select, back_routes.reshape(slot_total), preferre...]
    all_gather x2 -> x0, waiting for transfers between devices: 10 us -> none  [the longest x1 9.99 us: body(): lax.all_gather(out_grads[0], 'expert', axis=0, tiled=True)]
    all_to_all x2 -> x0, starting transfers between devices: 9.25 us -> none  [the longest x1 5.56 us: body(): lax.all_to_all(input_grad, 'expert', split_axis=1, concat_axis=0, tiled=T...]
    convert_element_type x7 -> x0, local copies, waits for them, and re-layouts: 9.1 us -> none  [the longest x1 4.93 us: expert_backward(): input_grad = (jnp.einsum('esh,edh->esd', gate_pre_grad, w_gate, preferred...]
  transfers between devices with their start and end apart: 5 -> 0, of which waited for: 2 -> 0; matrix products, arithmetic and copies ran while one was open for 34% -> 0% of each run, Pallas kernels for 0% -> 0%
where the time goes in v1:
time: 142 us
  Pallas kernels  129 us (91%)
  local copies, waits for them, and re-layouts  9.85 us (7%)
  other arithmetic  2.12 us (1%)
    pallas_call x1, Pallas kernels, body(): pl.pallas_call(functools.partial(kernel, lines, rows, sections), out_shap...  129 us
    unnamed x9, local copies, waits for them, and re-layouts  8.28 us

profile of v1, /device:TPU:1, one launch (start us, length us, event | category | flops | bytes accessed | tf_op | source)
XLA Modules:
  0.0 141.5 jit_solution(6210155421229271831)
XLA Ops:
  0.6 0.8 copy.14
  1.4 0.8 copy.15
  2.2 0.3 select_reduce_fusion.1
  2.6 0.6 multiply_convert_fusion.route_ref
  3.2 128.9 %shard_map.110 = (bf16[128,1024]{1,0:T(8,128)(2,1)}, bf16[128,128]{1,0:T(8,128)(2,1)}, bf16[2,1024,384]{2,1,0:T(8,128)(2,1)}, bf16[2,1024,384]{2,1,0:T(8,128)(2,1)}, bf16[2,384,1024]{2,1,0:T(8,128)(2,1)}) custom-call(bf16[128,1024]{1,0:T(8,128)(2,1)} %bitcast.20, bf16[128,1024]{1,0:T(8,128)(2,1)} %bitcast.21, ...), custom_call_target="tpu_custom_call" | custom-call | tf_op jit(solution)/shard_map/pallas_call | solution.py:276
  132.1 0.8 convert_element_type.25
  132.8 0.4 select_reduce_fusion
  133.2 0.7 copy.16
  133.9 1.7 %copy.21 = bf16[1,128,1024]{2,1,0:T(8,128)(2,1)} copy(bf16[1,128,1024]{2,1,0:T(8,128)(2,1)} %bitcast.22) | data formatting | bytes 524288
  135.6 0.0 copy-start.1
  135.6 2.8 %copy.22 = bf16[1,2,1024,384]{3,2,1,0:T(8,128)(2,1)} copy(bf16[1,2,1024,384]{3,2,1,0:T(8,128)(2,1)} %bitcast.16) | data formatting | bytes 3145728
  138.4 0.0 copy-done.1
  138.4 0.0 copy-start
  138.4 1.1 copy.23
  139.5 0.8 copy-done
  140.4 1.1 copy.24
Async XLA Ops:
  135.6 2.8 %copy-start.1 = (bf16[2,1024,384]{2,1,0:T(8,128)(2,1)S(1)}, bf16[2,1024,384]{2,1,0:T(8,128)(2,1)}, u32[]{:S(2)}) copy-start(bf16[2,1024,384]{2,1,0:T(8,128)(2,1)} %get-tuple-element.13) | copy-start | bytes 4718596
  138.4 2.0 %copy-start = (bf16[2,384,1024]{2,1,0:T(8,128)(2,1)S(1)}, bf16[2,384,1024]{2,1,0:T(8,128)(2,1)}, u32[]{:S(2)}) copy-start(bf16[2,384,1024]{2,1,0:T(8,128)(2,1)} %get-tuple-element.14) | copy-start | bytes 4718596

commit v2 on v1

--- a/solution.py
+++ b/solution.py
@@ -27,8 +27,14 @@
     section = lax.axis_index("section")
     z, x = me // rows, lax.rem(me, rows)
 
+    def paired(d):
+        if lines & (lines - 1):
+            return lax.rem(z + d, lines)
+        bits = lines.bit_length() - 1
+        return sum(((z // 2**i + d // 2**i) % 2) * 2**i for i in range(bits))
+
     def at(dz, dx):
-        return lax.rem(z + dz, lines) * rows + lax.rem(x + dx, rows)
+        return paired(dz) * rows + lax.rem(x + dx, rows)
 
     loads = [
         pltpu.make_async_copy(in_ref, packed.at[me, :, pl.ds(0, width)], load_sem.at[0]),
@@ -78,7 +84,7 @@
         ).wait_recv()
 
     def reduce_x(dz, dx):
-        line = lax.rem(z + dz, lines)
+        line = paired(dz)
         return pltpu.make_async_remote_copy(
             src_ref=x_out.at[line, dx - 1], dst_ref=x_in.at[line, dx - 1],
             send_sem=rx_send.at[line, dx - 1], recv_sem=rx_recv.at[line, dx - 1],
@@ -86,7 +92,7 @@
         )
 
     def reduce_z(dz):
-        line = lax.rem(z + dz, lines)
+        line = paired(dz)
         return pltpu.make_async_remote_copy(
             src_ref=z_out.at[line], dst_ref=z_in.at[dz],
             send_sem=rz_send.at[dz], recv_sem=rz_recv.at[dz],
@@ -137,7 +143,7 @@
         return total.astype(jnp.bfloat16), route_out.astype(jnp.bfloat16)
 
     def send_line(dz):
-        line = lax.rem(z + dz, lines)
+        line = paired(dz)
         for dx in range(1, rows):
             reduce_x(dz, dx).wait_recv()
         value = z_out[line].astype(jnp.float32)
@@ -148,7 +154,7 @@
     def step(j, carry):
         dz, dx = j // rows, lax.rem(j, rows)
         block = at(dz, dx)
-        line = lax.rem(z + dz, lines)
+        line = paired(dz)
 
         @pl.when(j > 0)
         def _():

time: 142 us -> 122 us (0.86)
  Pallas kernels: 129 us -> 109 us
    pallas_call x1, Pallas kernels: 129 us -> 109 us  [body(): pl.pallas_call(functools.partial(kernel, lines, rows, sections), out_shap...]
where the time goes in v2:
time: 122 us; the launch traced here: 121 us
  Pallas kernels  109 us (89%)
  local copies, waits for them, and re-layouts  9.85 us (8%)
  other arithmetic  2.12 us (2%)
    pallas_call x1, Pallas kernels, body(): pl.pallas_call(functools.partial(kernel, lines, rows, sections), out_shap...  109 us
    unnamed x9, local copies, waits for them, and re-layouts  8.28 us

profile of v2, /device:TPU:1, one launch (start us, length us, event | category | flops | bytes accessed | tf_op | source)
XLA Modules:
  0.0 121.3 jit_solution(10395897615972209978)
XLA Ops:
  0.6 0.8 copy.14
  1.4 0.8 copy.15
  2.2 0.3 select_reduce_fusion.1
  2.6 0.6 multiply_convert_fusion.route_ref
  3.2 108.7 %shard_map.110 = (bf16[128,1024]{1,0:T(8,128)(2,1)}, bf16[128,128]{1,0:T(8,128)(2,1)}, bf16[2,1024,384]{2,1,0:T(8,128)(2,1)}, bf16[2,1024,384]{2,1,0:T(8,128)(2,1)}, bf16[2,384,1024]{2,1,0:T(8,128)(2,1)}) custom-call(bf16[128,1024]{1,0:T(8,128)(2,1)} %bitcast.20, bf16[128,1024]{1,0:T(8,128)(2,1)} %bitcast.21, ...), custom_call_target="tpu_custom_call" | custom-call | tf_op jit(solution)/shard_map/pallas_call | solution.py:282
  111.8 0.8 convert_element_type.25
  112.6 0.4 select_reduce_fusion
  113.0 0.7 copy.16
  113.7 1.7 %copy.21 = bf16[1,128,1024]{2,1,0:T(8,128)(2,1)} copy(bf16[1,128,1024]{2,1,0:T(8,128)(2,1)} %bitcast.22) | data formatting | bytes 524288
  115.3 0.0 copy-start.1
  115.3 2.8 %copy.22 = bf16[1,2,1024,384]{3,2,1,0:T(8,128)(2,1)} copy(bf16[1,2,1024,384]{3,2,1,0:T(8,128)(2,1)} %bitcast.16) | data formatting | bytes 3145728
  118.2 0.0 copy-done.1
  118.2 0.0 copy-start
  118.2 1.1 copy.23
  119.3 0.8 copy-done
  120.1 1.1 copy.24
Async XLA Ops:
  115.3 2.8 %copy-start.1 = (bf16[2,1024,384]{2,1,0:T(8,128)(2,1)S(1)}, bf16[2,1024,384]{2,1,0:T(8,128)(2,1)}, u32[]{:S(2)}) copy-start(bf16[2,1024,384]{2,1,0:T(8,128)(2,1)} %get-tuple-element.13) | copy-start | bytes 4718596
  118.2 2.0 %copy-start = (bf16[2,384,1024]{2,1,0:T(8,128)(2,1)S(1)}, bf16[2,384,1024]{2,1,0:T(8,128)(2,1)}, u32[]{:S(2)}) copy-start(bf16[2,384,1024]{2,1,0:T(8,128)(2,1)} %get-tuple-element.14) | copy-start | bytes 4718596
